TPU v7x, 32 devices: a whole 2x2x4 slice. The times are simulated.
32 devices in a mesh: branch: 4 (over x, core), shard: 8 (over z, y).
Axes of the slice: x: 2, y: 2, z: 4, core: 2. Of those that a mesh axis runs over, the one named last changes fastest.
Arguments:
- attention_weights: bfloat16 [4, 2, 4096, 4096], P('branch', None, None, 'shard'), may hold values from -1.25 to 1.25
- ffn_weights: bfloat16 [4, 3, 4096, 11008], P('branch', None, 'shard'), may hold values from -0.3125 to 0.3125
- tokens: bfloat16 [512, 4096], P(('branch', 'shard')), may hold values from -6 to 6
- routes: int32 [512, 2], P(('branch', 'shard')), may hold values from 0 to 3, all different within a row; in each aligned block of 16 rows (0 to 15, 16 to 31, ...) at most 12 rows name the same one
- router: bfloat16 [4096, 4], replicated, may hold values from -0.09375 to 0.09375
Outputs:
- merged_attention: bfloat16 [2, 4096, 4096], P(None, 'branch', 'shard')
- expert_weights: bfloat16 [4, 3, 4096, 11008], P('branch', None, None, 'shard')
- mixed_output: bfloat16 [512, 4096], P(('branch', 'shard'))
Inputs may be any that keep to these rules, and one draw needn't show every extreme that they name: `routes`: the 2 experts of a row differ. In each aligned block of 16 rows (the rows of one device) no expert is named by more than 12 rows, and in some blocks one expert is named by exactly 12 rows.
All inputs are finite; a program needn't handle non-finite values.
Results may differ from a plain program's by a relative error of at most 0.018.
Values may be sent and summed in bfloat16 or wider, within the bound.
A program may use at most 256 MiB of HBM per device.

v0:
```python
import functools

import jax
import jax.numpy as jnp
from jax import lax
from jax.experimental import pallas as pl
from jax.experimental.pallas import tpu as pltpu
from jax.sharding import PartitionSpec as P

LANES = 128


def far_first(outer, inner):
    order = sorted(range(outer), key=lambda step: abs(2 * step - outer))
    return [(o, i) for o in order for i in range(inner - 1, -1, -1) if o or i]


def moved(place, step, outer, inner):
    return lax.rem(place // inner + step[0] + outer, outer) * inner + lax.rem(
        place % inner + step[1] + inner, inner
    )


def pack_kernel(info_ref, x_ref, after_ref, o_ref, turned_ref):
    turned_ref[...] = x_ref[0, 0].astype(turned_ref.dtype).T
    width = o_ref.shape[1]
    unit = 16 if turned_ref.dtype == jnp.bfloat16 else 8
    first = pl.multiple_of(info_ref[1], unit)
    o_ref[0] = turned_ref[pl.ds(first, width), :].astype(o_ref.dtype)


def pack(ffn, mats, rows, target, width, after):
    first, count = mats
    low, height = rows
    ff = ffn.shape[3]
    window = min(-(-(width + LANES - 1) // LANES) * LANES, ff)
    start = jnp.minimum(target * width // LANES, (ff - window) // LANES)
    tile = max(t for t in (2 * LANES, LANES) if height % t == 0)
    kind = jnp.bfloat16 if width % 16 == 0 else jnp.float32
    return pl.pallas_call(
        pack_kernel,
        grid_spec=pltpu.PrefetchScalarGridSpec(
            num_scalar_prefetch=1,
            grid=(count, height // tile),
            in_specs=[
                pl.BlockSpec(
                    (pl.Element(1), pl.Element(1), pl.Element(tile), pl.Element(window)),
                    lambda m, r, t: (
                        0,
                        m + first,
                        pl.multiple_of(low + r * tile, LANES),
                        pl.multiple_of(t[0] * LANES, LANES),
                    ),
                ),
                pl.BlockSpec(memory_space=pl.ANY),
            ],
            out_specs=pl.BlockSpec((1, width, tile), lambda m, r, t: (m, 0, r)),
            scratch_shapes=[pltpu.VMEM((window, tile), kind)],
        ),
        out_shape=jax.ShapeDtypeStruct((count, width, height), ffn.dtype),
        cost_estimate=pl.CostEstimate(
            flops=0, bytes_accessed=5 * count * height * width, transcendentals=0
        ),
    )(jnp.stack([start, target * width - start * LANES]).astype(jnp.int32), ffn, after)


def gate_up_kernel(info_ref, rows_ref, piece_ref, *refs):
    total_ref, out_ref = refs[-2:]
    total = lax.dot_general(
        rows_ref[...], piece_ref[0], (((1,), (1,)), ((), ())), preferred_element_type=jnp.float32
    )
    total_ref[0] = refs[0][0] + total if len(refs) > 2 else total
    out_ref[0] = piece_ref[0]


def gate_up_step(all_rows, source, piece, carried, shape):
    count, width, depth = piece.shape
    rows = all_rows.shape[0]
    total_spec = pl.BlockSpec((1, rows, width), lambda m, t: (m, 0, 0))
    return pl.pallas_call(
        gate_up_kernel,
        grid_spec=pltpu.PrefetchScalarGridSpec(
            num_scalar_prefetch=1,
            grid=(count,),
            in_specs=[
                pl.BlockSpec((rows, depth), lambda m, t: (0, t[0])),
                pl.BlockSpec((1, width, depth), lambda m, t: (m, 0, 0)),
            ]
            + [total_spec, pl.BlockSpec(memory_space=pl.ANY)][: len(carried)],
            out_specs=[total_spec, pl.BlockSpec((1, width, depth), lambda m, t: (m, 0, t[0]))],
        ),
        out_shape=[
            jax.ShapeDtypeStruct((count, rows, width), jnp.float32),
            jax.ShapeDtypeStruct(shape, piece.dtype),
        ],
        input_output_aliases={3 + i: i for i in range(len(carried))},
        cost_estimate=pl.CostEstimate(
            flops=2 * count * rows * depth * width,
            bytes_accessed=count * width * (4 * depth + 8 * rows),
            transcendentals=0,
        ),
    )(jnp.stack([source]).astype(jnp.int32), all_rows, piece, *carried)


def down_kernel(steps, sizes, low, hidden_ref, weight_ref, *refs):
    pieces, (partial_ref, out_ref, sems) = refs[: len(steps)], refs[-3:]
    me = lax.axis_index("shard")
    last = out_ref.shape[0] - 1
    height = pieces[0].shape[2]
    depth = out_ref.shape[2] // partial_ref.shape[0]
    copies = []
    for k, (step, piece_ref) in enumerate(zip(steps, pieces)):
        columns = pl.ds(pl.multiple_of(moved(me, step, *sizes) * depth + low, LANES), height)
        copy = pltpu.make_async_copy(piece_ref.at[0], out_ref.at[last, :, columns], sems.at[k])
        copy.start()
        copies.append(copy)
    for step, piece_ref in zip(steps, pieces):
        columns = jnp.dot(hidden_ref[...], piece_ref[0], preferred_element_type=jnp.float32)
        partial_ref[moved(me, step, *sizes)] = (columns * weight_ref[...]).astype(partial_ref.dtype)
    for copy in copies:
        copy.wait()


def down(hidden, weight, steps, sizes, pieces, low, weights):
    _, width, height = pieces[0].shape
    rows, shards = hidden.shape[0], len(pieces)
    return pl.pallas_call(
        functools.partial(down_kernel, steps, sizes, low),
        grid=(1,),
        in_specs=[
            pl.BlockSpec((rows, width), lambda i: (0, 0)),
            pl.BlockSpec((rows, 1), lambda i: (0, 0)),
        ]
        + [pl.BlockSpec((1, width, height), lambda i: (0, 0, 0))] * shards
        + [pl.BlockSpec(memory_space=pl.ANY)],
        out_specs=[
            pl.BlockSpec((shards, rows, height), lambda i: (0, 0, 0)),
            pl.BlockSpec(memory_space=pl.ANY),
        ],
        out_shape=[
            jax.ShapeDtypeStruct((shards, rows, height), jnp.bfloat16),
            jax.ShapeDtypeStruct(weights.shape, weights.dtype),
        ],
        scratch_shapes=[pltpu.SemaphoreType.DMA((shards,))],
        input_output_aliases={2 + shards: 1},
        cost_estimate=pl.CostEstimate(
            flops=2 * rows * height * width * shards,
            bytes_accessed=shards * height * (4 * width + 2 * rows) + 2 * rows * width,
            transcendentals=0,
        ),
    )(hidden, weight, *pieces, weights)


def from_ahead(x, step, outer, inner):
    pairs = [
        (((o + step[0]) % outer) * inner + (i + step[1]) % inner, o * inner + i)
        for o in range(outer)
        for i in range(inner)
    ]
    return lax.ppermute(x, "shard", pairs)


def from_branch(x, step):
    count = lax.axis_size("branch")
    return lax.ppermute(x, "branch", [((b + step) % count, b) for b in range(count)])


def gather_all(x, outer, inner):
    x = jnp.concatenate([x] + [from_ahead(x, (k, 0), outer, inner) for k in range(1, outer)])
    x = jnp.concatenate([x] + [from_ahead(x, (0, k), outer, inner) for k in range(1, inner)])
    others = range(1, lax.axis_size("branch"))
    return jnp.concatenate([x] + [from_branch(x, k) for k in others])


def add_up(pieces):
    return functools.reduce(lambda a, b: a + b, [p.astype(jnp.float32) for p in pieces])


def scatter_sum(x, outer, inner):
    def stage(x, count, move):
        parts = jnp.split(x, count, axis=1)
        return add_up([parts[0]] + [move(parts[k], count - k) for k in range(1, count)])

    x = stage(x, lax.axis_size("branch"), from_branch).astype(jnp.bfloat16)
    move = lambda p, k: from_ahead(p, (0, k), outer, inner)
    x = stage(x, inner, move).astype(jnp.bfloat16)
    move = lambda p, k: from_ahead(p, (k, 0), outer, inner)
    return stage(x, outer, move).astype(jnp.bfloat16)


def local(attention_weights, ffn_weights, tokens, routes, router):
    branches = lax.axis_size("branch")
    shards = lax.axis_size("shard")
    inner = 2 if shards % 2 == 0 else 1
    outer = shards // inner
    me = lax.axis_index("shard")
    expert = lax.axis_index("branch")
    every, depth = ffn_weights.shape[1:3]
    width = ffn_weights.shape[3] // shards
    model_width = shards * depth
    own_rows = tokens.shape[0]

    chosen = jnp.any(routes[:, :, None] == jnp.arange(branches, dtype=jnp.int32), axis=1)
    chosen = jnp.pad(chosen.astype(tokens.dtype), ((0, 0), (0, LANES - branches)))
    all_rows = gather_all(jnp.concatenate([tokens, chosen], axis=1), outer, inner)

    low = max(depth - LANES, 0)
    groups = [((0, 2), (0, depth))]
    groups += [((2, 1), rows) for rows in ((0, low), (low, depth - low)) if rows[1]]
    order = far_first(outer, inner)
    backs = [(0, 0)] + [(outer - o, inner - i) for o, i in order]
    after = routes
    own, arrivals, number = [], [], 0
    for mats, rows in groups:
        pieces = []
        for step in order:
            after = pack(ffn_weights, mats, rows, moved(me, step, outer, inner), width, after)
            pieces.append(from_ahead(after, (outer - step[0], inner - step[1]), outer, inner))
            number += 1
        arrivals.append(pieces)
    for mats, rows in groups:
        own.append(pack(ffn_weights, mats, rows, me, width, after))

    gates = jax.nn.sigmoid(
        jnp.dot(all_rows[:, :model_width], router, preferred_element_type=jnp.float32)
    )
    picked = all_rows[:, model_width : model_width + branches].astype(jnp.float32)
    mine = (jnp.arange(branches) == expert).astype(jnp.float32)
    weight = jnp.sum(gates * picked * mine, axis=1, keepdims=True)

    carried = ()
    shape = (every, width, model_width)
    for at, piece in enumerate([own[0]] + arrivals[0]):
        source = moved(me, backs[at], outer, inner)
        carried = gate_up_step(all_rows, source, piece, carried, shape)
    total, weights = carried
    hidden = (jax.nn.silu(total[0]) * total[1]).astype(jnp.bfloat16)

    mixed = []
    for group in range(1, len(groups)):
        pieces = [own[group]] + arrivals[group]
        partial, weights = down(
            hidden, weight, backs, (outer, inner), pieces, groups[group][1][0], weights
        )
        mixed.append(scatter_sum(partial, outer, inner))
    mixed_output = jnp.concatenate(mixed, axis=2).transpose(1, 0, 2).reshape(own_rows, model_width)
    expert_weights = weights.transpose(0, 2, 1)[None]

    share = attention_weights.shape[2] // branches
    pieces = []
    for step in range(branches):
        rows = lax.rem(expert + step, branches) * share
        block = lax.dynamic_slice_in_dim(attention_weights[0], rows, share, 1)
        pieces.append(from_branch(block, branches - step) if step else block)
    merged_attention = (add_up(pieces) * (1.0 / branches)).astype(jnp.bfloat16)
    return (merged_attention, expert_weights, mixed_output)


def solution(mesh):
    placed = (
        P("branch", None, None, "shard"),
        P("branch", None, "shard", None),
        P(("branch", "shard"), None),
        P(("branch", "shard"), None),
        P(),
    )
    return jax.shard_map(
        local,
        mesh=mesh,
        in_specs=placed,
        out_specs=(
            P(None, "branch", "shard"),
            P("branch", None, None, "shard"),
            P(("branch", "shard"), None),
        ),
        check_vma=False,
    )
```

profile of v0, /device:TPU:0, one launch (start us, length us, event | category | flops | bytes accessed | tf_op | source)
XLA Modules:
  0.0 971.4 jit_solution(7577377354361362568)
XLA Ops:
  3.7 5.1 collective-permute-start.3
  13.1 5.3 shard_map.76.after_ref
  18.4 5.4 shard_map.77.after_ref
  23.8 5.4 shard_map.78.after_ref
  29.2 5.4 shard_map.79.after_ref
  34.6 5.4 shard_map.80.after_ref
  40.6 5.4 shard_map.81.after_ref
  46.0 5.4 shard_map.82.after_ref
  51.3 4.0 shard_map.83.after_ref
  55.4 4.0 shard_map.84.after_ref
  59.4 4.1 shard_map.85.after_ref
  63.4 4.0 shard_map.86.after_ref
  67.5 4.0 shard_map.87.after_ref
  71.5 4.0 shard_map.88.after_ref
  75.5 4.0 shard_map.89.after_ref
  79.5 2.6 shard_map.90.after_ref
  82.1 2.6 shard_map.91.after_ref
  84.7 2.6 shard_map.92.after_ref
  87.3 2.6 shard_map.93.after_ref
  89.9 2.6 shard_map.94.after_ref
  92.5 3.8 collective-permute-start.21
  96.2 2.6 shard_map.95.after_ref
  99.4 2.7 shard_map.96.after_ref
  109.4 4.6 collective-permute-done.23.refs_7_
  114.0 3.6 collective-permute-start.16
  117.6 11.7 %collective-permute-start.15 = (bf16[2,1376,512]{2,1,0:T(8,128)(2,1)}, bf16[2,1376,512]{2,1,0:T(8,128)(2,1)}, u32[]{:S(2)}, u32[]{:S(2)}) collective-permute-start(bf16[2,1376,512]{2,1,0:T(8,128)(2,1)} %shard_map.77.after_ref), channel_id=1, source_target_pairs={{4,0},{5,1},{6,2},{7,3},{0,4},{1,5},{2,6},{3,7},{12,8},{13,9},{14,... | collective-permute-start | bytes 8454152 | tf_op jit(solution)/shard_map/ppermute | solution.py:160
  129.8 3.9 collective-permute-start.29
  136.9 22.9 %collective-permute-done.6 = bf16[64,4224]{1,0:T(8,128)(2,1)S(1)} collective-permute-done((bf16[64,4224]{1,0:T(8,128)(2,1)S(1)}, bf16[64,4224]{1,0:T(8,128)(2,1)S(1)}, u32[]{:S(2)}, u32[]{:S(2)}) %collective-permute-start.6) | collective-permute-done | bytes 540704 | tf_op jit(solution)/shard_map/ppermute | solution.py:160
  159.9 2.8 collective-permute-start.28
  163.7 107.6 %collective-permute-done.29.refs_6_ = bf16[1,1376,384]{2,1,0:T(8,128)(2,1)S(1)} collective-permute-done((bf16[1,1376,384]{2,1,0:T(8,128)(2,1)S(1)}, bf16[1,1376,384]{2,1,0:T(8,128)(2,1)S(1)}, u32[]{:S(2)}, u32[]{:S(2)}) %collective-permute-start.29) | collective-permute-done | bytes 1056800 | tf_op jit(solution)/shard_map/ppermute | solution.py:160
  272.8 19.5 %collective-permute-done.28.refs_5_ = bf16[1,1376,384]{2,1,0:T(8,128)(2,1)S(1)} collective-permute-done((bf16[1,1376,384]{2,1,0:T(8,128)(2,1)S(1)}, bf16[1,1376,384]{2,1,0:T(8,128)(2,1)S(1)}, u32[]{:S(2)}, u32[]{:S(2)}) %collective-permute-start.28) | collective-permute-done | bytes 1056800 | tf_op jit(solution)/shard_map/ppermute | solution.py:160
  293.2 183.8 %collective-permute-start.14 = (bf16[2,1376,512]{2,1,0:T(8,128)(2,1)}, bf16[2,1376,512]{2,1,0:T(8,128)(2,1)}, u32[]{:S(2)}, u32[]{:S(2)}) collective-permute-start(bf16[2,1376,512]{2,1,0:T(8,128)(2,1)} %shard_map.78.after_ref), channel_id=1, source_target_pairs={{7,0},{6,1},{1,2},{0,3},{3,4},{2,5},{5,6},{4,7},{15,8},{14,9},{9,1... | collective-permute-start | bytes 8454152 | tf_op jit(solution)/shard_map/ppermute | solution.py:160
  479.2 5.5 shard_map.97.piece_ref
  484.7 4.0 shard_map.107.refs_0_
  488.7 2.6 shard_map.106.refs_0_
  491.3 5.8 dynamic-slice_bitcast_fusion.2
  507.9 31.1 %collective-permute-done.14.piece_ref = bf16[2,1376,512]{2,1,0:T(8,128)(2,1)} collective-permute-done((bf16[2,1376,512]{2,1,0:T(8,128)(2,1)}, bf16[2,1376,512]{2,1,0:T(8,128)(2,1)}, u32[]{:S(2)}, u32[]{:S(2)}) %collective-permute-start.14) | collective-permute-done | bytes 2818080 | tf_op jit(solution)/shard_map/ppermute | solution.py:160
  539.0 2.4 collective-permute-start.27
  541.4 58.0 %collective-permute-done.13.piece_ref = bf16[2,1376,512]{2,1,0:T(8,128)(2,1)} collective-permute-done((bf16[2,1376,512]{2,1,0:T(8,128)(2,1)}, bf16[2,1376,512]{2,1,0:T(8,128)(2,1)}, u32[]{:S(2)}, u32[]{:S(2)}) %collective-permute-start.13) | collective-permute-done | bytes 2818080 | tf_op jit(solution)/shard_map/ppermute | solution.py:160
  599.4 2.4 collective-permute-start.26
  601.8 3.5 fusion.28
  606.2 5.9 shard_map.98
  612.1 6.9 shard_map.99
  619.0 6.9 shard_map.100
  625.8 6.9 shard_map.101
  632.7 6.9 shard_map.102
  639.5 103.3 %collective-permute-done.27.refs_4_ = bf16[1,1376,384]{2,1,0:T(8,128)(2,1)} collective-permute-done((bf16[1,1376,384]{2,1,0:T(8,128)(2,1)}, bf16[1,1376,384]{2,1,0:T(8,128)(2,1)}, u32[]{:S(2)}, u32[]{:S(2)}) %collective-permute-start.27) | collective-permute-done | bytes 1056800 | tf_op jit(solution)/shard_map/ppermute | solution.py:160
  745.7 6.9 shard_map.103
  752.6 12.9 %collective-permute-done.26.refs_3_ = bf16[1,1376,384]{2,1,0:T(8,128)(2,1)} collective-permute-done((bf16[1,1376,384]{2,1,0:T(8,128)(2,1)}, bf16[1,1376,384]{2,1,0:T(8,128)(2,1)}, u32[]{:S(2)}, u32[]{:S(2)}) %collective-permute-start.26) | collective-permute-done | bytes 1056800 | tf_op jit(solution)/shard_map/ppermute | solution.py:160
  768.5 6.8 shard_map.104
  775.3 6.9 shard_map.105
  782.2 4.7 fusion.6.hidden_ref
  786.8 28.7 %collective-permute-done.25.refs_2_ = bf16[1,1376,384]{2,1,0:T(8,128)(2,1)} collective-permute-done((bf16[1,1376,384]{2,1,0:T(8,128)(2,1)}, bf16[1,1376,384]{2,1,0:T(8,128)(2,1)}, u32[]{:S(2)}, u32[]{:S(2)}) %collective-permute-start.25) | collective-permute-done | bytes 1056800 | tf_op jit(solution)/shard_map/ppermute | solution.py:160
  815.6 22.6 %collective-permute-done.24.refs_1_ = bf16[1,1376,384]{2,1,0:T(8,128)(2,1)} collective-permute-done((bf16[1,1376,384]{2,1,0:T(8,128)(2,1)}, bf16[1,1376,384]{2,1,0:T(8,128)(2,1)}, u32[]{:S(2)}, u32[]{:S(2)}) %collective-permute-start.24) | collective-permute-done | bytes 1056800 | tf_op jit(solution)/shard_map/ppermute | solution.py:160
  838.2 14.3 %shard_map.108 = (bf16[8,512,384]{2,1,0:T(8,128)(2,1)}, bf16[3,1376,4096]{2,1,0:T(8,128)(2,1)}) custom-call(bf16[512,1376]{1,0:T(8,128)(2,1)} %fusion.6.hidden_ref, f32[512,1]{1,0:T(8,128)} %copy.45.weight_ref, bf16[1,1376,384]{2,1,0:T(8,128)(2,1)} %shard_map.107.refs_0_, ...), custom_call_target="tpu_custom_call", output_to_operand_aliasing={{1}: (10, {})} | custom-call | flops 4328521728 | bytes 21463040 | tf_op jit(solution)/shard_map/pallas_call | solution.py:127
  853.3 8.0 shard_map.109
  869.3 6.0 fusion.5
  875.3 33.3 %collective-permute-done.39 = bf16[8,128,128]{2,1,0:T(8,128)(2,1)S(1)} collective-permute-done((bf16[8,128,128]{2,1,0:T(8,128)(2,1)}, bf16[8,128,128]{2,1,0:T(8,128)(2,1)S(1)}, u32[]{:S(2)}, u32[]{:S(2)}) %collective-permute-start.39) | collective-permute-done | bytes 262176 | tf_op jit(solution)/shard_map/ppermute | solution.py:165
  910.8 7.7 collective-permute-start.41
  921.5 32.7 %collective-permute-start.42 = (bf16[8,16,128]{2,1,0:T(8,128)(2,1)S(1)}, bf16[8,16,128]{2,1,0:T(8,128)(2,1)S(1)}, u32[]{:S(2)}, u32[]{:S(2)}) collective-permute-start(bf16[8,16,128]{2,1,0:T(8,128)(2,1)S(1)} %get-tuple-element.66), channel_id=1, source_target_pairs={{6,0},{7,1},{0,2},{1,3},{2,4},{3,5},{4,6},{5,7},{14,8},{15,9},{8,1... | collective-permute-start | bytes 98312 | tf_op jit(solution)/shard_map/ppermute | solution.py:160
  954.2 2.4 collective-permute-start.44
  956.8 6.5 collective-permute-start.35
  963.3 2.4 collective-permute-start.37
  966.4 4.2 collective-permute-done.36
  (132 shorter events, 58.3 us)
Async XLA Ops:
  0.6 601.2 %copy-start = (bf16[4096,4]{0,1:T(4,128)(2,1)S(1)}, bf16[4096,4]{0,1:T(4,128)(2,1)}, u32[]{:S(2)}) copy-start(bf16[4096,4]{0,1:T(4,128)(2,1)} %param.9) | copy-start | bytes 98308
  1.5 0.6 copy-start.16
  3.7 98.4 %collective-permute-start.3 = (bf16[16,4224]{1,0:T(8,128)(2,1)}, bf16[16,4224]{1,0:T(8,128)(2,1)}, u32[]{:S(2)}, u32[]{:S(2)}) collective-permute-start(bf16[16,4224]{1,0:T(8,128)(2,1)} %get-tuple-element.65), channel_id=1, source_target_pairs={{2,0},{3,1},{4,2},{5,3},{6,4},{7,5},{0,6},{1,7},{10,8},{11,9},{12,... | collective-permute-start | bytes 405512 | tf_op jit(solution)/shard_map/ppermute | solution.py:160
  8.8 96.3 %collective-permute-start.4 = (bf16[16,4224]{1,0:T(8,128)(2,1)}, bf16[16,4224]{1,0:T(8,128)(2,1)}, u32[]{:S(2)}, u32[]{:S(2)}) collective-permute-start(bf16[16,4224]{1,0:T(8,128)(2,1)} %get-tuple-element.65), channel_id=1, source_target_pairs={{4,0},{5,1},{6,2},{7,3},{0,4},{1,5},{2,6},{3,7},{12,8},{13,9},{14,... | collective-permute-start | bytes 405512 | tf_op jit(solution)/shard_map/ppermute | solution.py:160
  8.8 96.3 %collective-permute-start.5 = (bf16[16,4224]{1,0:T(8,128)(2,1)}, bf16[16,4224]{1,0:T(8,128)(2,1)}, u32[]{:S(2)}, u32[]{:S(2)}) collective-permute-start(bf16[16,4224]{1,0:T(8,128)(2,1)} %get-tuple-element.65), channel_id=1, source_target_pairs={{6,0},{7,1},{0,2},{1,3},{2,4},{3,5},{4,6},{5,7},{14,8},{15,9},{8,1... | collective-permute-start | bytes 405512 | tf_op jit(solution)/shard_map/ppermute | solution.py:160
  92.5 36.8 %collective-permute-start.21 = (bf16[1,1376,128]{2,1,0:T(8,128)(2,1)}, bf16[1,1376,128]{2,1,0:T(8,128)(2,1)}, u32[]{:S(2)}, u32[]{:S(2)}) collective-permute-start(bf16[1,1376,128]{2,1,0:T(8,128)(2,1)} %shard_map.94.after_ref), channel_id=1, source_target_pairs={{3,0},{2,1},{5,2},{4,3},{7,4},{6,5},{1,6},{0,7},{11,8},{10,9},{13,... | collective-permute-start | bytes 1056776 | tf_op jit(solution)/shard_map/ppermute | solution.py:160
  98.8 6.3 copy-start.8
  98.8 30.5 %copy-start.4 = (bf16[1,1376,384]{2,1,0:T(8,128)(2,1)S(1)}, bf16[1,1376,384]{2,1,0:T(8,128)(2,1)}, u32[]{:S(2)}) copy-start(bf16[1,1376,384]{2,1,0:T(8,128)(2,1)} %shard_map.89.after_ref) | copy-start | bytes 3170308
  98.8 31.0 %copy-start.3 = (bf16[1,1376,384]{2,1,0:T(8,128)(2,1)S(1)}, bf16[1,1376,384]{2,1,0:T(8,128)(2,1)}, u32[]{:S(2)}) copy-start(bf16[1,1376,384]{2,1,0:T(8,128)(2,1)} %shard_map.88.after_ref) | copy-start | bytes 3170308
  98.8 61.1 %copy-start.2 = (bf16[1,1376,384]{2,1,0:T(8,128)(2,1)S(1)}, bf16[1,1376,384]{2,1,0:T(8,128)(2,1)}, u32[]{:S(2)}) copy-start(bf16[1,1376,384]{2,1,0:T(8,128)(2,1)} %shard_map.87.after_ref) | copy-start | bytes 3170308
  98.8 18.8 %collective-permute-start.22 = (bf16[1,1376,128]{2,1,0:T(8,128)(2,1)}, bf16[1,1376,128]{2,1,0:T(8,128)(2,1)}, u32[]{:S(2)}, u32[]{:S(2)}) collective-permute-start(bf16[1,1376,128]{2,1,0:T(8,128)(2,1)} %shard_map.95.after_ref), channel_id=1, source_target_pairs={{2,0},{3,1},{4,2},{5,3},{6,4},{7,5},{0,6},{1,7},{10,8},{11,9},{12,... | collective-permute-start | bytes 1056776 | tf_op jit(solution)/shard_map/ppermute | solution.py:160
  102.1 27.7 %collective-permute-start.20 = (bf16[1,1376,128]{2,1,0:T(8,128)(2,1)}, bf16[1,1376,128]{2,1,0:T(8,128)(2,1)}, u32[]{:S(2)}, u32[]{:S(2)}) collective-permute-start(bf16[1,1376,128]{2,1,0:T(8,128)(2,1)} %shard_map.93.after_ref), channel_id=1, source_target_pairs={{6,0},{7,1},{0,2},{1,3},{2,4},{3,5},{4,6},{5,7},{14,8},{15,9},{8,1... | collective-permute-start | bytes 1056776 | tf_op jit(solution)/shard_map/ppermute | solution.py:160
  105.1 28.6 %collective-permute-start.19 = (bf16[1,1376,128]{2,1,0:T(8,128)(2,1)S(1)}, bf16[1,1376,128]{2,1,0:T(8,128)(2,1)S(1)}, u32[]{:S(2)}, u32[]{:S(2)}) collective-permute-start(bf16[1,1376,128]{2,1,0:T(8,128)(2,1)S(1)} %copy-done.8), channel_id=1, source_target_pairs={{7,0},{6,1},{1,2},{0,3},{3,4},{2,5},{5,6},{4,7},{15,8},{14,9},{9,1... | collective-permute-start | bytes 1056776 | tf_op jit(solution)/shard_map/ppermute | solution.py:160
  105.2 8.9 collective-permute-start.23
  114.0 15.8 %copy-start.13 = (bf16[1,1376,128]{2,1,0:T(8,128)(2,1)}, bf16[1,1376,128]{2,1,0:T(8,128)(2,1)S(1)}, u32[]{:S(2)}) copy-start(bf16[1,1376,128]{2,1,0:T(8,128)(2,1)S(1)} %collective-permute-done.23.refs_7_) | copy-start | bytes 1056772
  114.0 385.3 %collective-permute-start.16 = (bf16[2,1376,512]{2,1,0:T(8,128)(2,1)}, bf16[2,1376,512]{2,1,0:T(8,128)(2,1)}, u32[]{:S(2)}, u32[]{:S(2)}) collective-permute-start(bf16[2,1376,512]{2,1,0:T(8,128)(2,1)} %shard_map.76.after_ref), channel_id=1, source_target_pairs={{5,0},{4,1},{7,2},{6,3},{1,4},{0,5},{3,6},{2,7},{13,8},{12,9},{15,... | collective-permute-start | bytes 8454152 | tf_op jit(solution)/shard_map/ppermute | solution.py:160
  117.6 381.9 %collective-permute-start.15 = (bf16[2,1376,512]{2,1,0:T(8,128)(2,1)}, bf16[2,1376,512]{2,1,0:T(8,128)(2,1)}, u32[]{:S(2)}, u32[]{:S(2)}) collective-permute-start(bf16[2,1376,512]{2,1,0:T(8,128)(2,1)} %shard_map.77.after_ref), channel_id=1, source_target_pairs={{4,0},{5,1},{6,2},{7,3},{0,4},{1,5},{2,6},{3,7},{12,8},{13,9},{14,... | collective-permute-start | bytes 8454152 | tf_op jit(solution)/shard_map/ppermute | solution.py:160
  129.3 34.4 %collective-permute-start.30 = (bf16[1,1376,384]{2,1,0:T(8,128)(2,1)S(1)}, bf16[1,1376,384]{2,1,0:T(8,128)(2,1)S(1)}, u32[]{:S(2)}, u32[]{:S(2)}) collective-permute-start(bf16[1,1376,384]{2,1,0:T(8,128)(2,1)S(1)} %copy-done.4), channel_id=1, source_target_pairs={{1,0},{0,1},{3,2},{2,3},{5,4},{4,5},{7,6},{6,7},{9,8},{8,9},{11,10... | collective-permute-start | bytes 3170312 | tf_op jit(solution)/shard_map/ppermute | solution.py:160
  129.8 141.4 %collective-permute-start.29 = (bf16[1,1376,384]{2,1,0:T(8,128)(2,1)S(1)}, bf16[1,1376,384]{2,1,0:T(8,128)(2,1)S(1)}, u32[]{:S(2)}, u32[]{:S(2)}) collective-permute-start(bf16[1,1376,384]{2,1,0:T(8,128)(2,1)S(1)} %copy-done.3), channel_id=1, source_target_pairs={{2,0},{3,1},{4,2},{5,3},{6,4},{7,5},{0,6},{1,7},{10,8},{11,9},{12,... | collective-permute-start | bytes 3170312 | tf_op jit(solution)/shard_map/ppermute | solution.py:160
  133.8 3.2 copy-start.12
  133.8 26.1 %collective-permute-start.6 = (bf16[64,4224]{1,0:T(8,128)(2,1)S(1)}, bf16[64,4224]{1,0:T(8,128)(2,1)S(1)}, u32[]{:S(2)}, u32[]{:S(2)}) collective-permute-start(bf16[64,4224]{1,0:T(8,128)(2,1)S(1)} %pad_maximum_fusion), channel_id=1, source_target_pairs={{1,0},{0,1},{3,2},{2,3},{5,4},{4,5},{7,6},{6,7},{9,8},{8,9},{11,10... | collective-permute-start | bytes 1622024 | tf_op jit(solution)/shard_map/ppermute | solution.py:160
  159.9 132.4 %collective-permute-start.28 = (bf16[1,1376,384]{2,1,0:T(8,128)(2,1)S(1)}, bf16[1,1376,384]{2,1,0:T(8,128)(2,1)S(1)}, u32[]{:S(2)}, u32[]{:S(2)}) collective-permute-start(bf16[1,1376,384]{2,1,0:T(8,128)(2,1)S(1)} %copy-done.2), channel_id=1, source_target_pairs={{3,0},{2,1},{5,2},{4,3},{7,4},{6,5},{1,6},{0,7},{11,8},{10,9},{13,... | collective-permute-start | bytes 3170312 | tf_op jit(solution)/shard_map/ppermute | solution.py:160
  163.7 128.5 %copy-start.9 = (bf16[1,1376,384]{2,1,0:T(8,128)(2,1)}, bf16[1,1376,384]{2,1,0:T(8,128)(2,1)S(1)}, u32[]{:S(2)}) copy-start(bf16[1,1376,384]{2,1,0:T(8,128)(2,1)S(1)} %collective-permute-done.30.refs_7_) | copy-start | bytes 3170308
  163.7 128.5 %collective-permute-start.7 = (bf16[128,4224]{1,0:T(8,128)(2,1)}, bf16[128,4224]{1,0:T(8,128)(2,1)}, u32[]{:S(2)}, u32[]{:S(2)}) collective-permute-start(bf16[128,4224]{1,0:T(8,128)(2,1)} %get-tuple-element.52), channel_id=1, source_target_pairs={{8,0},{16,8},{24,16},{0,24},{9,1},{17,9},{25,17},{1,25},{10,2},{18... | collective-permute-start | bytes 3244040 | tf_op jit(solution)/shard_map/ppermute | solution.py:165
  271.3 21.0 %copy-start.10 = (bf16[1,1376,384]{2,1,0:T(8,128)(2,1)}, bf16[1,1376,384]{2,1,0:T(8,128)(2,1)S(1)}, u32[]{:S(2)}) copy-start(bf16[1,1376,384]{2,1,0:T(8,128)(2,1)S(1)} %collective-permute-done.29.refs_6_) | copy-start | bytes 3170308
  271.3 205.8 %collective-permute-start.8 = (bf16[128,4224]{1,0:T(8,128)(2,1)}, bf16[128,4224]{1,0:T(8,128)(2,1)}, u32[]{:S(2)}, u32[]{:S(2)}) collective-permute-start(bf16[128,4224]{1,0:T(8,128)(2,1)} %get-tuple-element.52), channel_id=1, source_target_pairs={{16,0},{24,8},{0,16},{8,24},{17,1},{25,9},{1,17},{9,25},{18,2},{26... | collective-permute-start | bytes 3244040 | tf_op jit(solution)/shard_map/ppermute | solution.py:165
  292.2 1.0 copy-start.11
  292.2 204.9 %collective-permute-start.9 = (bf16[128,4224]{1,0:T(8,128)(2,1)}, bf16[128,4224]{1,0:T(8,128)(2,1)}, u32[]{:S(2)}, u32[]{:S(2)}) collective-permute-start(bf16[128,4224]{1,0:T(8,128)(2,1)} %get-tuple-element.52), channel_id=1, source_target_pairs={{24,0},{0,8},{8,16},{16,24},{25,1},{1,9},{9,17},{17,25},{26,2},{2,... | collective-permute-start | bytes 3244040 | tf_op jit(solution)/shard_map/ppermute | solution.py:165
  293.2 245.8 %collective-permute-start.14 = (bf16[2,1376,512]{2,1,0:T(8,128)(2,1)}, bf16[2,1376,512]{2,1,0:T(8,128)(2,1)}, u32[]{:S(2)}, u32[]{:S(2)}) collective-permute-start(bf16[2,1376,512]{2,1,0:T(8,128)(2,1)} %shard_map.78.after_ref), channel_id=1, source_target_pairs={{7,0},{6,1},{1,2},{0,3},{3,4},{2,5},{5,6},{4,7},{15,8},{14,9},{9,1... | collective-permute-start | bytes 8454152 | tf_op jit(solution)/shard_map/ppermute | solution.py:160
  477.1 122.3 %collective-permute-start.13 = (bf16[2,1376,512]{2,1,0:T(8,128)(2,1)}, bf16[2,1376,512]{2,1,0:T(8,128)(2,1)}, u32[]{:S(2)}, u32[]{:S(2)}) collective-permute-start(bf16[2,1376,512]{2,1,0:T(8,128)(2,1)} %shard_map.79.after_ref), channel_id=1, source_target_pairs={{6,0},{7,1},{0,2},{1,3},{2,4},{3,5},{4,6},{5,7},{14,8},{15,9},{8,1... | collective-permute-start | bytes 8454152 | tf_op jit(solution)/shard_map/ppermute | solution.py:160
  491.3 8.2 copy-start.1
  497.2 246.5 %collective-permute-start.12 = (bf16[2,1376,512]{2,1,0:T(8,128)(2,1)}, bf16[2,1376,512]{2,1,0:T(8,128)(2,1)}, u32[]{:S(2)}, u32[]{:S(2)}) collective-permute-start(bf16[2,1376,512]{2,1,0:T(8,128)(2,1)} %shard_map.80.after_ref), channel_id=1, source_target_pairs={{3,0},{2,1},{5,2},{4,3},{7,4},{6,5},{1,6},{0,7},{11,8},{10,9},{13,... | collective-permute-start | bytes 8454152 | tf_op jit(solution)/shard_map/ppermute | solution.py:160
  499.4 266.1 %collective-permute-start.11 = (bf16[2,1376,512]{2,1,0:T(8,128)(2,1)}, bf16[2,1376,512]{2,1,0:T(8,128)(2,1)}, u32[]{:S(2)}, u32[]{:S(2)}) collective-permute-start(bf16[2,1376,512]{2,1,0:T(8,128)(2,1)} %shard_map.81.after_ref), channel_id=1, source_target_pairs={{2,0},{3,1},{4,2},{5,3},{6,4},{7,5},{0,6},{1,7},{10,8},{11,9},{12,... | collective-permute-start | bytes 8454152 | tf_op jit(solution)/shard_map/ppermute | solution.py:160
  499.5 267.5 %collective-permute-start.10 = (bf16[2,1376,512]{2,1,0:T(8,128)(2,1)S(1)}, bf16[2,1376,512]{2,1,0:T(8,128)(2,1)}, u32[]{:S(2)}, u32[]{:S(2)}) collective-permute-start(bf16[2,1376,512]{2,1,0:T(8,128)(2,1)S(1)} %copy-done.1), channel_id=1, source_target_pairs={{1,0},{0,1},{3,2},{2,3},{5,4},{4,5},{7,6},{6,7},{9,8},{8,9},{11,10... | collective-permute-start | bytes 8454152 | tf_op jit(solution)/shard_map/ppermute | solution.py:160
  539.0 203.9 %collective-permute-start.27 = (bf16[1,1376,384]{2,1,0:T(8,128)(2,1)}, bf16[1,1376,384]{2,1,0:T(8,128)(2,1)}, u32[]{:S(2)}, u32[]{:S(2)}) collective-permute-start(bf16[1,1376,384]{2,1,0:T(8,128)(2,1)} %shard_map.86.after_ref), channel_id=1, source_target_pairs={{6,0},{7,1},{0,2},{1,3},{2,4},{3,5},{4,6},{5,7},{14,8},{15,9},{8,1... | collective-permute-start | bytes 3170312 | tf_op jit(solution)/shard_map/ppermute | solution.py:160
  599.4 166.1 %collective-permute-start.26 = (bf16[1,1376,384]{2,1,0:T(8,128)(2,1)}, bf16[1,1376,384]{2,1,0:T(8,128)(2,1)}, u32[]{:S(2)}, u32[]{:S(2)}) collective-permute-start(bf16[1,1376,384]{2,1,0:T(8,128)(2,1)} %shard_map.85.after_ref), channel_id=1, source_target_pairs={{7,0},{6,1},{1,2},{0,3},{3,4},{2,5},{5,6},{4,7},{15,8},{14,9},{9,1... | collective-permute-start | bytes 3170312 | tf_op jit(solution)/shard_map/ppermute | solution.py:160
  742.9 72.7 %collective-permute-start.25 = (bf16[1,1376,384]{2,1,0:T(8,128)(2,1)}, bf16[1,1376,384]{2,1,0:T(8,128)(2,1)}, u32[]{:S(2)}, u32[]{:S(2)}) collective-permute-start(bf16[1,1376,384]{2,1,0:T(8,128)(2,1)} %shard_map.84.after_ref), channel_id=1, source_target_pairs={{4,0},{5,1},{6,2},{7,3},{0,4},{1,5},{2,6},{3,7},{12,8},{13,9},{14,... | collective-permute-start | bytes 3170312 | tf_op jit(solution)/shard_map/ppermute | solution.py:160
  743.7 94.5 %collective-permute-start.24 = (bf16[1,1376,384]{2,1,0:T(8,128)(2,1)}, bf16[1,1376,384]{2,1,0:T(8,128)(2,1)}, u32[]{:S(2)}, u32[]{:S(2)}) collective-permute-start(bf16[1,1376,384]{2,1,0:T(8,128)(2,1)} %shard_map.83.after_ref), channel_id=1, source_target_pairs={{5,0},{4,1},{7,2},{6,3},{1,4},{0,5},{3,6},{2,7},{13,8},{12,9},{15,... | collective-permute-start | bytes 3170312 | tf_op jit(solution)/shard_map/ppermute | solution.py:160
  765.5 100.1 %collective-permute-start = (bf16[2,1024,512]{2,1,0:T(8,128)(2,1)}, bf16[2,1024,512]{2,1,0:T(8,128)(2,1)}, u32[]{:S(2)}, u32[]{:S(2)}) collective-permute-start(bf16[2,1024,512]{2,1,0:T(8,128)(2,1)} %get-tuple-element.43), channel_id=1, source_target_pairs={{24,0},{0,8},{8,16},{16,24},{25,1},{1,9},{9,17},{17,25},{26,2},{2,... | collective-permute-start | bytes 6291464 | tf_op jit(solution)/shard_map/ppermute | solution.py:165
  765.5 101.5 %collective-permute-start.1 = (bf16[2,1024,512]{2,1,0:T(8,128)(2,1)}, bf16[2,1024,512]{2,1,0:T(8,128)(2,1)}, u32[]{:S(2)}, u32[]{:S(2)}) collective-permute-start(bf16[2,1024,512]{2,1,0:T(8,128)(2,1)} %get-tuple-element.45), channel_id=1, source_target_pairs={{16,0},{24,8},{0,16},{8,24},{17,1},{25,9},{1,17},{9,25},{18,2},{26... | collective-permute-start | bytes 6291464 | tf_op jit(solution)/shard_map/ppermute | solution.py:165
  767.0 100.0 %collective-permute-start.2 = (bf16[2,1024,512]{2,1,0:T(8,128)(2,1)}, bf16[2,1024,512]{2,1,0:T(8,128)(2,1)}, u32[]{:S(2)}, u32[]{:S(2)}) collective-permute-start(bf16[2,1024,512]{2,1,0:T(8,128)(2,1)} %get-tuple-element.44), channel_id=1, source_target_pairs={{8,0},{16,8},{24,16},{0,24},{9,1},{17,9},{25,17},{1,25},{10,2},{18... | collective-permute-start | bytes 6291464 | tf_op jit(solution)/shard_map/ppermute | solution.py:165
  782.2 33.4 %copy-start.7 = (bf16[1,1376,128]{2,1,0:T(8,128)(2,1)S(1)}, bf16[1,1376,128]{2,1,0:T(8,128)(2,1)}, u32[]{:S(2)}) copy-start(bf16[1,1376,128]{2,1,0:T(8,128)(2,1)} %shard_map.91.after_ref) | copy-start | bytes 1056772
  782.2 56.0 %copy-start.6 = (bf16[1,1376,128]{2,1,0:T(8,128)(2,1)S(1)}, bf16[1,1376,128]{2,1,0:T(8,128)(2,1)}, u32[]{:S(2)}) copy-start(bf16[1,1376,128]{2,1,0:T(8,128)(2,1)} %shard_map.90.after_ref) | copy-start | bytes 1056772
  815.6 36.9 %collective-permute-start.18 = (bf16[1,1376,128]{2,1,0:T(8,128)(2,1)S(1)}, bf16[1,1376,128]{2,1,0:T(8,128)(2,1)S(1)}, u32[]{:S(2)}, u32[]{:S(2)}) collective-permute-start(bf16[1,1376,128]{2,1,0:T(8,128)(2,1)S(1)} %copy-done.7), channel_id=1, source_target_pairs={{4,0},{5,1},{6,2},{7,3},{0,4},{1,5},{2,6},{3,7},{12,8},{13,9},{14,... | collective-permute-start | bytes 1056776 | tf_op jit(solution)/shard_map/ppermute | solution.py:160
  838.2 14.3 %collective-permute-start.17 = (bf16[1,1376,128]{2,1,0:T(8,128)(2,1)S(1)}, bf16[1,1376,128]{2,1,0:T(8,128)(2,1)S(1)}, u32[]{:S(2)}, u32[]{:S(2)}) collective-permute-start(bf16[1,1376,128]{2,1,0:T(8,128)(2,1)S(1)} %copy-done.6), channel_id=1, source_target_pairs={{5,0},{4,1},{7,2},{6,3},{1,4},{0,5},{3,6},{2,7},{13,8},{12,9},{15,... | collective-permute-start | bytes 1056776 | tf_op jit(solution)/shard_map/ppermute | solution.py:160
  852.4 0.9 copy-start.14
  852.5 0.8 copy-start.15
  853.3 10.0 %copy-start.5 = (bf16[8,512,384]{2,1,0:T(8,128)(2,1)S(1)}, bf16[8,512,384]{2,1,0:T(8,128)(2,1)}, u32[]{:S(2)}) copy-start(bf16[8,512,384]{2,1,0:T(8,128)(2,1)} %get-tuple-element.41) | copy-start | bytes 9437188
  863.3 6.0 collective-permute-start.38
  864.9 53.6 %collective-permute-start.31 = (bf16[8,128,384]{2,1,0:T(8,128)(2,1)}, bf16[8,128,384]{2,1,0:T(8,128)(2,1)}, u32[]{:S(2)}, u32[]{:S(2)}) collective-permute-start(bf16[8,128,384]{2,1,0:T(8,128)(2,1)} %get-tuple-element.46), channel_id=1, source_target_pairs={{24,0},{0,8},{8,16},{16,24},{25,1},{1,9},{9,17},{17,25},{26,2},{2,... | collective-permute-start | bytes 2359304 | tf_op jit(solution)/shard_map/ppermute | solution.py:165
  865.6 52.9 %collective-permute-start.32 = (bf16[8,128,384]{2,1,0:T(8,128)(2,1)}, bf16[8,128,384]{2,1,0:T(8,128)(2,1)}, u32[]{:S(2)}, u32[]{:S(2)}) collective-permute-start(bf16[8,128,384]{2,1,0:T(8,128)(2,1)} %get-tuple-element.48), channel_id=1, source_target_pairs={{16,0},{24,8},{0,16},{8,24},{17,1},{25,9},{1,17},{9,25},{18,2},{26... | collective-permute-start | bytes 2359304 | tf_op jit(solution)/shard_map/ppermute | solution.py:165
  867.0 51.4 %collective-permute-start.33 = (bf16[8,128,384]{2,1,0:T(8,128)(2,1)}, bf16[8,128,384]{2,1,0:T(8,128)(2,1)}, u32[]{:S(2)}, u32[]{:S(2)}) collective-permute-start(bf16[8,128,384]{2,1,0:T(8,128)(2,1)} %get-tuple-element.47), channel_id=1, source_target_pairs={{8,0},{16,8},{24,16},{0,24},{9,1},{17,9},{25,17},{1,25},{10,2},{18... | collective-permute-start | bytes 2359304 | tf_op jit(solution)/shard_map/ppermute | solution.py:165
  867.0 41.6 %collective-permute-start.39 = (bf16[8,128,128]{2,1,0:T(8,128)(2,1)}, bf16[8,128,128]{2,1,0:T(8,128)(2,1)S(1)}, u32[]{:S(2)}, u32[]{:S(2)}) collective-permute-start(bf16[8,128,128]{2,1,0:T(8,128)(2,1)} %get-tuple-element.51), channel_id=1, source_target_pairs={{16,0},{24,8},{0,16},{8,24},{17,1},{25,9},{1,17},{9,25},{18,2},{26... | collective-permute-start | bytes 786440 | tf_op jit(solution)/shard_map/ppermute | solution.py:165
  869.3 40.3 %collective-permute-start.40 = (bf16[8,128,128]{2,1,0:T(8,128)(2,1)}, bf16[8,128,128]{2,1,0:T(8,128)(2,1)S(1)}, u32[]{:S(2)}, u32[]{:S(2)}) collective-permute-start(bf16[8,128,128]{2,1,0:T(8,128)(2,1)} %get-tuple-element.50), channel_id=1, source_target_pairs={{8,0},{16,8},{24,16},{0,24},{9,1},{17,9},{25,17},{1,25},{10,2},{18... | collective-permute-start | bytes 786440 | tf_op jit(solution)/shard_map/ppermute | solution.py:165
  910.8 10.7 %collective-permute-start.41 = (bf16[8,64,128]{2,1,0:T(8,128)(2,1)S(1)}, bf16[8,64,128]{2,1,0:T(8,128)(2,1)S(1)}, u32[]{:S(2)}, u32[]{:S(2)}) collective-permute-start(bf16[8,64,128]{2,1,0:T(8,128)(2,1)S(1)} %split.87), channel_id=1, source_target_pairs={{1,0},{0,1},{3,2},{2,3},{5,4},{4,5},{7,6},{6,7},{9,8},{8,9},{11,10... | collective-permute-start | bytes 393224 | tf_op jit(solution)/shard_map/ppermute | solution.py:160
  920.5 36.1 %collective-permute-start.34 = (bf16[8,64,384]{2,1,0:T(8,128)(2,1)S(1)}, bf16[8,64,384]{2,1,0:T(8,128)(2,1)S(1)}, u32[]{:S(2)}, u32[]{:S(2)}) collective-permute-start(bf16[8,64,384]{2,1,0:T(8,128)(2,1)S(1)} %split.81), channel_id=1, source_target_pairs={{1,0},{0,1},{3,2},{2,3},{5,4},{4,5},{7,6},{6,7},{9,8},{8,9},{11,10... | collective-permute-start | bytes 1179656 | tf_op jit(solution)/shard_map/ppermute | solution.py:160
  921.5 41.8 %collective-permute-start.42 = (bf16[8,16,128]{2,1,0:T(8,128)(2,1)S(1)}, bf16[8,16,128]{2,1,0:T(8,128)(2,1)S(1)}, u32[]{:S(2)}, u32[]{:S(2)}) collective-permute-start(bf16[8,16,128]{2,1,0:T(8,128)(2,1)S(1)} %get-tuple-element.66), channel_id=1, source_target_pairs={{6,0},{7,1},{0,2},{1,3},{2,4},{3,5},{4,6},{5,7},{14,8},{15,9},{8,1... | collective-permute-start | bytes 98312 | tf_op jit(solution)/shard_map/ppermute | solution.py:160
  954.2 11.5 %collective-permute-start.43 = (bf16[8,16,128]{2,1,0:T(8,128)(2,1)S(1)}, bf16[8,16,128]{2,1,0:T(8,128)(2,1)S(1)}, u32[]{:S(2)}, u32[]{:S(2)}) collective-permute-start(bf16[8,16,128]{2,1,0:T(8,128)(2,1)S(1)} %get-tuple-element.68), channel_id=1, source_target_pairs={{4,0},{5,1},{6,2},{7,3},{0,4},{1,5},{2,6},{3,7},{12,8},{13,9},{14,... | collective-permute-start | bytes 98312 | tf_op jit(solution)/shard_map/ppermute | solution.py:160
  954.2 11.5 %collective-permute-start.44 = (bf16[8,16,128]{2,1,0:T(8,128)(2,1)S(1)}, bf16[8,16,128]{2,1,0:T(8,128)(2,1)S(1)}, u32[]{:S(2)}, u32[]{:S(2)}) collective-permute-start(bf16[8,16,128]{2,1,0:T(8,128)(2,1)S(1)} %get-tuple-element.67), channel_id=1, source_target_pairs={{2,0},{3,1},{4,2},{5,3},{6,4},{7,5},{0,6},{1,7},{10,8},{11,9},{12,... | collective-permute-start | bytes 98312 | tf_op jit(solution)/shard_map/ppermute | solution.py:160
  956.8 9.7 collective-permute-start.35
  963.3 7.4 collective-permute-start.36
  963.3 7.4 collective-permute-start.37
where the time goes:
time: 973 us; the launch traced here: 971 us
  waiting for transfers between devices  452 us (46%)
  starting transfers between devices  294 us (30%)
  Pallas kernels  172 us (18%)
  local copies, waits for them, and re-layouts  27.9 us (3%)
  other arithmetic  20.7 us (2%)
    ppermute x33, waiting for transfers between devices, from_ahead(): return lax.ppermute(x, 'shard', pairs)  417 us
    ppermute x33, starting transfers between devices, from_ahead(): return lax.ppermute(x, 'shard', pairs)  286 us
    pallas_call x24, Pallas kernels, pack(): pl.pallas_call(pack_kernel, grid_spec=pltpu.PrefetchScalarGridSpec(num_sc...  96.1 us
    pallas_call x8, Pallas kernels, gate_up_step(): pl.pallas_call(gate_up_kernel, grid_spec=pltpu.PrefetchScalarGridSpec(num...  53.9 us
    ppermute x12, waiting for transfers between devices, from_branch(): lax.ppermute(x, 'branch', [((b + step) % count, b) for b in range(count)])  35.3 us
    pallas_call x2, Pallas kernels, down(): pl.pallas_call(functools.partial(down_kernel, steps, sizes, low), grid=(1...  22.2 us
  transfers between devices with their start and end apart: 45, of which 16 were waited for; matrix products, arithmetic and copies ran while one was open for 5% of the time, Pallas kernels for 18%

commit v1 on v0

--- a/solution.py
+++ b/solution.py
@@ -151,13 +151,13 @@
     )(hidden, weight, *pieces, weights)
 
 
-def from_ahead(x, step, outer, inner):
+def from_ahead(x, step, outer, inner, axis="shard"):
     pairs = [
         (((o + step[0]) % outer) * inner + (i + step[1]) % inner, o * inner + i)
         for o in range(outer)
         for i in range(inner)
     ]
-    return lax.ppermute(x, "shard", pairs)
+    return lax.ppermute(x, axis, pairs)
 
 
 def from_branch(x, step):
@@ -165,11 +165,20 @@
     return lax.ppermute(x, "branch", [((b + step) % count, b) for b in range(count)])
 
 
+def branch_sizes():
+    count = lax.axis_size("branch")
+    cores = 2 if count % 2 == 0 else 1
+    return count // cores, cores
+
+
 def gather_all(x, outer, inner):
     x = jnp.concatenate([x] + [from_ahead(x, (k, 0), outer, inner) for k in range(1, outer)])
     x = jnp.concatenate([x] + [from_ahead(x, (0, k), outer, inner) for k in range(1, inner)])
-    others = range(1, lax.axis_size("branch"))
-    return jnp.concatenate([x] + [from_branch(x, k) for k in others])
+    chips, cores = branch_sizes()
+    moves = [((k, 0), chips, cores, "branch") for k in range(1, chips)]
+    x = jnp.concatenate([x] + [from_ahead(x, *move) for move in moves])
+    moves = [((0, k), chips, cores, "branch") for k in range(1, cores)]
+    return jnp.concatenate([x] + [from_ahead(x, *move) for move in moves])
 
 
 def add_up(pieces):
@@ -181,7 +190,11 @@
         parts = jnp.split(x, count, axis=1)
         return add_up([parts[0]] + [move(parts[k], count - k) for k in range(1, count)])
 
-    x = stage(x, lax.axis_size("branch"), from_branch).astype(jnp.bfloat16)
+    chips, cores = branch_sizes()
+    move = lambda p, k: from_ahead(p, (0, k), chips, cores, "branch")
+    x = stage(x, cores, move).astype(jnp.bfloat16)
+    move = lambda p, k: from_ahead(p, (k, 0), chips, cores, "branch")
+    x = stage(x, chips, move).astype(jnp.bfloat16)
     move = lambda p, k: from_ahead(p, (0, k), outer, inner)
     x = stage(x, inner, move).astype(jnp.bfloat16)
     move = lambda p, k: from_ahead(p, (k, 0), outer, inner)

time: 973 us -> 928 us (0.954)
  starting transfers between devices: 294 us -> 150 us
  waiting for transfers between devices: 452 us -> 554 us
    ppermute x33 -> x39, starting transfers between devices: 286 us -> 148 us  [from_ahead(): return lax.ppermute(x, axis, pairs)]
    ppermute x33 -> x39, waiting for transfers between devices: 417 us -> 533 us  [from_ahead(): return lax.ppermute(x, axis, pairs)]
    ppermute x12 -> x3, waiting for transfers between devices: 35.3 us -> 21.2 us  [from_branch(): lax.ppermute(x, 'branch', [((b + step) % count, b) for b in range(count)])]
  transfers between devices with their start and end apart: 45 -> 42, of which waited for: 16 -> 20; matrix products, arithmetic and copies ran while one was open for 5% -> 4% of each run, Pallas kernels for 18% -> 19%
where the time goes in v1:
time: 928 us; the launch traced here: 926 us
  waiting for transfers between devices  554 us (60%)
  Pallas kernels  172 us (19%)
  starting transfers between devices  150 us (16%)
  local copies, waits for them, and re-layouts  24.2 us (3%)
  other arithmetic  20.6 us (2%)
    ppermute x39, waiting for transfers between devices, from_ahead(): return lax.ppermute(x, axis, pairs)  533 us
    ppermute x39, starting transfers between devices, from_ahead(): return lax.ppermute(x, axis, pairs)  148 us
    pallas_call x24, Pallas kernels, pack(): pl.pallas_call(pack_kernel, grid_spec=pltpu.PrefetchScalarGridSpec(num_sc...  96.1 us
    pallas_call x8, Pallas kernels, gate_up_step(): pl.pallas_call(gate_up_kernel, grid_spec=pltpu.PrefetchScalarGridSpec(num...  54 us
    pallas_call x2, Pallas kernels, down(): pl.pallas_call(functools.partial(down_kernel, steps, sizes, low), grid=(1...  22.2 us
    ppermute x3, waiting for transfers between devices, from_branch(): lax.ppermute(x, 'branch', [((b + step) % count, b) for b in range(count)])  21.2 us
  transfers between devices with their start and end apart: 42, of which 20 were waited for; matrix products, arithmetic and copies ran while one was open for 4% of the time, Pallas kernels for 19%

profile of v1, /device:TPU:0, one launch (start us, length us, event | category | flops | bytes accessed | tf_op | source)
XLA Modules:
  0.0 925.9 jit_solution(18194966966127313105)
XLA Ops:
  3.1 5.1 collective-permute-start.3
  9.2 3.0 collective-permute-done.3
  12.2 7.5 collective-permute-done.4
  24.4 9.9 %collective-permute-done.6 = bf16[64,4224]{1,0:T(8,128)(2,1)S(1)} collective-permute-done((bf16[64,4224]{1,0:T(8,128)(2,1)S(1)}, bf16[64,4224]{1,0:T(8,128)(2,1)S(1)}, u32[]{:S(2)}, u32[]{:S(2)}) %collective-permute-start.6) | collective-permute-done | bytes 540704 | tf_op jit(solution)/shard_map/ppermute | solution.py:160
  39.4 5.3 shard_map.76.after_ref
  44.8 3.5 collective-permute-start.15
  48.9 5.4 shard_map.77.after_ref
  54.7 6.6 collective-permute-done.7
  61.4 2.8 constant_dynamic-update-slice_fusion.5
  64.1 5.4 shard_map.78.after_ref
  71.6 5.4 shard_map.79.after_ref
  79.5 5.4 shard_map.80.after_ref
  85.5 5.5 shard_map.81.after_ref
  91.0 5.4 shard_map.82.after_ref
  96.3 253.3 %collective-permute-done.15.piece_ref = bf16[2,1376,512]{2,1,0:T(8,128)(2,1)S(1)} collective-permute-done((bf16[2,1376,512]{2,1,0:T(8,128)(2,1)}, bf16[2,1376,512]{2,1,0:T(8,128)(2,1)S(1)}, u32[]{:S(2)}, u32[]{:S(2)}) %collective-permute-start.15) | collective-permute-done | bytes 2818080 | tf_op jit(solution)/shard_map/ppermute | solution.py:160
  349.6 60.6 %collective-permute-done.14.piece_ref = bf16[2,1376,512]{2,1,0:T(8,128)(2,1)} collective-permute-done((bf16[2,1376,512]{2,1,0:T(8,128)(2,1)}, bf16[2,1376,512]{2,1,0:T(8,128)(2,1)}, u32[]{:S(2)}, u32[]{:S(2)}) %collective-permute-start.14) | collective-permute-done | bytes 2818080 | tf_op jit(solution)/shard_map/ppermute | solution.py:160
  410.7 4.0 shard_map.83.after_ref
  414.8 4.1 shard_map.84.after_ref
  418.8 4.0 shard_map.85.after_ref
  422.9 4.0 shard_map.86.after_ref
  426.9 4.0 shard_map.87.after_ref
  430.9 4.0 shard_map.88.after_ref
  435.0 4.0 shard_map.89.after_ref
  444.1 2.6 shard_map.92.after_ref
  457.6 5.4 shard_map.97.piece_ref
  463.0 4.1 shard_map.107.refs_0_
  467.1 3.1 constant_dynamic-update-slice_fusion.11.rows_ref
  472.7 6.0 shard_map.98
  478.7 6.9 shard_map.99
  485.6 6.9 shard_map.100
  492.4 6.9 shard_map.101
  499.3 6.9 shard_map.102
  506.2 3.7 fusion.28
  509.8 43.6 %collective-permute-done.29.refs_7_ = bf16[1,1376,384]{2,1,0:T(8,128)(2,1)} collective-permute-done((bf16[1,1376,384]{2,1,0:T(8,128)(2,1)}, bf16[1,1376,384]{2,1,0:T(8,128)(2,1)}, u32[]{:S(2)}, u32[]{:S(2)}) %collective-permute-start.29) | collective-permute-done | bytes 1056800 | tf_op jit(solution)/shard_map/ppermute | solution.py:160
  553.5 38.1 %collective-permute-start.27 = (bf16[1,1376,384]{2,1,0:T(8,128)(2,1)}, bf16[1,1376,384]{2,1,0:T(8,128)(2,1)}, u32[]{:S(2)}, u32[]{:S(2)}) collective-permute-start(bf16[1,1376,384]{2,1,0:T(8,128)(2,1)} %shard_map.87.after_ref), channel_id=1, source_target_pairs={{3,0},{2,1},{5,2},{4,3},{7,4},{6,5},{1,6},{0,7},{11,8},{10,9},{13,... | collective-permute-start | bytes 3170312 | tf_op jit(solution)/shard_map/ppermute | solution.py:160
  591.7 4.6 collective-permute-start.24
  597.0 6.8 shard_map.103
  604.7 6.8 shard_map.104
  611.5 6.9 shard_map.105
  618.4 4.7 fusion.6.hidden_ref
  623.9 14.9 %collective-permute-done.26.refs_4_ = bf16[1,1376,384]{2,1,0:T(8,128)(2,1)} collective-permute-done((bf16[1,1376,384]{2,1,0:T(8,128)(2,1)S(1)}, bf16[1,1376,384]{2,1,0:T(8,128)(2,1)}, u32[]{:S(2)}, u32[]{:S(2)}) %collective-permute-start.26) | collective-permute-done | bytes 1056800 | tf_op jit(solution)/shard_map/ppermute | solution.py:160
  638.8 22.9 %collective-permute-done.25.refs_3_ = bf16[1,1376,384]{2,1,0:T(8,128)(2,1)} collective-permute-done((bf16[1,1376,384]{2,1,0:T(8,128)(2,1)S(1)}, bf16[1,1376,384]{2,1,0:T(8,128)(2,1)}, u32[]{:S(2)}, u32[]{:S(2)}) %collective-permute-start.25) | collective-permute-done | bytes 1056800 | tf_op jit(solution)/shard_map/ppermute | solution.py:160
  661.8 43.0 %collective-permute-start.20 = (bf16[1,1376,128]{2,1,0:T(8,128)(2,1)}, bf16[1,1376,128]{2,1,0:T(8,128)(2,1)S(1)}, u32[]{:S(2)}, u32[]{:S(2)}) collective-permute-start(bf16[1,1376,128]{2,1,0:T(8,128)(2,1)} %shard_map.94.after_ref), channel_id=1, source_target_pairs={{3,0},{2,1},{5,2},{4,3},{7,4},{6,5},{1,6},{0,7},{11,8},{10,9},{13,... | collective-permute-start | bytes 1056776 | tf_op jit(solution)/shard_map/ppermute | solution.py:160
  704.7 22.7 %collective-permute-done.24.refs_2_ = bf16[1,1376,384]{2,1,0:T(8,128)(2,1)} collective-permute-done((bf16[1,1376,384]{2,1,0:T(8,128)(2,1)S(1)}, bf16[1,1376,384]{2,1,0:T(8,128)(2,1)}, u32[]{:S(2)}, u32[]{:S(2)}) %collective-permute-start.24) | collective-permute-done | bytes 1056800 | tf_op jit(solution)/shard_map/ppermute | solution.py:160
  727.5 13.9 %collective-permute-start.19 = (bf16[1,1376,128]{2,1,0:T(8,128)(2,1)}, bf16[1,1376,128]{2,1,0:T(8,128)(2,1)S(1)}, u32[]{:S(2)}, u32[]{:S(2)}) collective-permute-start(bf16[1,1376,128]{2,1,0:T(8,128)(2,1)} %shard_map.93.after_ref), channel_id=1, source_target_pairs={{6,0},{7,1},{0,2},{1,3},{2,4},{3,5},{4,6},{5,7},{14,8},{15,9},{8,1... | collective-permute-start | bytes 1056776 | tf_op jit(solution)/shard_map/ppermute | solution.py:160
  741.3 16.8 %collective-permute-done.23.refs_1_ = bf16[1,1376,384]{2,1,0:T(8,128)(2,1)} collective-permute-done((bf16[1,1376,384]{2,1,0:T(8,128)(2,1)}, bf16[1,1376,384]{2,1,0:T(8,128)(2,1)}, u32[]{:S(2)}, u32[]{:S(2)}) %collective-permute-start.23) | collective-permute-done | bytes 1056800 | tf_op jit(solution)/shard_map/ppermute | solution.py:160
  758.1 14.2 %shard_map.108 = (bf16[8,512,384]{2,1,0:T(8,128)(2,1)}, bf16[3,1376,4096]{2,1,0:T(8,128)(2,1)}) custom-call(bf16[512,1376]{1,0:T(8,128)(2,1)} %fusion.6.hidden_ref, f32[512,1]{1,0:T(8,128)} %copy.45.weight_ref, bf16[1,1376,384]{2,1,0:T(8,128)(2,1)} %shard_map.107.refs_0_, ...), custom_call_target="tpu_custom_call", output_to_operand_aliasing={{1}: (10, {})} | custom-call | flops 4328521728 | bytes 21463040 | tf_op jit(solution)/shard_map/pallas_call | solution.py:127
  772.4 2.7 split.61
  775.1 5.8 dynamic-slice_bitcast_fusion.2
  782.9 5.6 collective-permute-start.18
  788.6 12.4 %collective-permute-done.18.refs_3_ = bf16[1,1376,128]{2,1,0:T(8,128)(2,1)S(1)} collective-permute-done((bf16[1,1376,128]{2,1,0:T(8,128)(2,1)S(1)}, bf16[1,1376,128]{2,1,0:T(8,128)(2,1)S(1)}, u32[]{:S(2)}, u32[]{:S(2)}) %collective-permute-start.18) | collective-permute-done | bytes 352288 | tf_op jit(solution)/shard_map/ppermute | solution.py:160
  801.0 16.3 %collective-permute-done.17.refs_2_ = bf16[1,1376,128]{2,1,0:T(8,128)(2,1)S(1)} collective-permute-done((bf16[1,1376,128]{2,1,0:T(8,128)(2,1)S(1)}, bf16[1,1376,128]{2,1,0:T(8,128)(2,1)S(1)}, u32[]{:S(2)}, u32[]{:S(2)}) %collective-permute-start.17) | collective-permute-done | bytes 352288 | tf_op jit(solution)/shard_map/ppermute | solution.py:160
  818.0 2.6 shard_map.106.refs_0_
  820.7 15.3 %collective-permute-done.16.refs_1_ = bf16[1,1376,128]{2,1,0:T(8,128)(2,1)S(1)} collective-permute-done((bf16[1,1376,128]{2,1,0:T(8,128)(2,1)S(1)}, bf16[1,1376,128]{2,1,0:T(8,128)(2,1)S(1)}, u32[]{:S(2)}, u32[]{:S(2)}) %collective-permute-start.16) | collective-permute-done | bytes 352288 | tf_op jit(solution)/shard_map/ppermute | solution.py:160
  836.7 7.9 shard_map.109
  851.9 21.2 %collective-permute-done.2 = bf16[2,1024,512]{2,1,0:T(8,128)(2,1)} collective-permute-done((bf16[2,1024,512]{2,1,0:T(8,128)(2,1)}, bf16[2,1024,512]{2,1,0:T(8,128)(2,1)}, u32[]{:S(2)}, u32[]{:S(2)}) %collective-permute-start.2) | collective-permute-done | bytes 2097184 | tf_op jit(solution)/shard_map/ppermute | solution.py:165
  873.1 6.0 fusion.5
  879.1 17.3 %collective-permute-done.37 = bf16[8,128,128]{2,1,0:T(8,128)(2,1)S(1)} collective-permute-done((bf16[8,128,128]{2,1,0:T(8,128)(2,1)S(1)}, bf16[8,128,128]{2,1,0:T(8,128)(2,1)S(1)}, u32[]{:S(2)}, u32[]{:S(2)}) %collective-permute-start.37) | collective-permute-done | bytes 262176 | tf_op jit(solution)/shard_map/ppermute | solution.py:160
  899.0 4.0 collective-permute-done.38
  903.0 6.0 collective-permute-start.39
  909.1 2.9 collective-permute-start.40
  912.2 3.6 collective-permute-start.33
  915.7 3.4 collective-permute-start.34
  919.2 3.1 collective-permute-done.33
  (133 shorter events, 58.1 us)
Async XLA Ops:
  0.6 505.5 %copy-start = (bf16[4096,4]{0,1:T(4,128)(2,1)S(1)}, bf16[4096,4]{0,1:T(4,128)(2,1)}, u32[]{:S(2)}) copy-start(bf16[4096,4]{0,1:T(4,128)(2,1)} %param.9) | copy-start | bytes 98308
  3.1 9.1 collective-permute-start.3
  8.2 11.5 %collective-permute-start.4 = (bf16[16,4224]{1,0:T(8,128)(2,1)S(1)}, bf16[16,4224]{1,0:T(8,128)(2,1)S(1)}, u32[]{:S(2)}, u32[]{:S(2)}) collective-permute-start(bf16[16,4224]{1,0:T(8,128)(2,1)S(1)} %get-tuple-element.66), channel_id=1, source_target_pairs={{4,0},{5,1},{6,2},{7,3},{0,4},{1,5},{2,6},{3,7},{12,8},{13,9},{14,... | collective-permute-start | bytes 405512 | tf_op jit(solution)/shard_map/ppermute | solution.py:160
  8.2 11.5 %collective-permute-start.5 = (bf16[16,4224]{1,0:T(8,128)(2,1)S(1)}, bf16[16,4224]{1,0:T(8,128)(2,1)S(1)}, u32[]{:S(2)}, u32[]{:S(2)}) collective-permute-start(bf16[16,4224]{1,0:T(8,128)(2,1)S(1)} %get-tuple-element.66), channel_id=1, source_target_pairs={{6,0},{7,1},{0,2},{1,3},{2,4},{3,5},{4,6},{5,7},{14,8},{15,9},{8,1... | collective-permute-start | bytes 405512 | tf_op jit(solution)/shard_map/ppermute | solution.py:160
  20.6 17.6 %copy-start.18 = (s32[16,2]{0,1:T(2,128)S(1)}, s32[16,2]{0,1:T(2,128)}, u32[]{:S(2)}) copy-start(s32[16,2]{0,1:T(2,128)} %param.8) | copy-start | bytes 388
  20.7 13.7 %collective-permute-start.6 = (bf16[64,4224]{1,0:T(8,128)(2,1)S(1)}, bf16[64,4224]{1,0:T(8,128)(2,1)S(1)}, u32[]{:S(2)}, u32[]{:S(2)}) collective-permute-start(bf16[64,4224]{1,0:T(8,128)(2,1)S(1)} %pad_maximum_fusion), channel_id=1, source_target_pairs={{1,0},{0,1},{3,2},{2,3},{5,4},{4,5},{7,6},{6,7},{9,8},{8,9},{11,10... | collective-permute-start | bytes 1622024 | tf_op jit(solution)/shard_map/ppermute | solution.py:160
  35.4 1.3 copy-start.17
  36.7 24.6 %collective-permute-start.7 = (bf16[128,4224]{1,0:T(8,128)(2,1)}, bf16[128,4224]{1,0:T(8,128)(2,1)}, u32[]{:S(2)}, u32[]{:S(2)}) collective-permute-start(bf16[128,4224]{1,0:T(8,128)(2,1)} %get-tuple-element.50), channel_id=1, source_target_pairs={{16,0},{24,8},{0,16},{8,24},{17,1},{25,9},{1,17},{9,25},{18,2},{26... | collective-permute-start | bytes 3244040 | tf_op jit(solution)/shard_map/ppermute | solution.py:160
  44.8 304.9 %collective-permute-start.15 = (bf16[2,1376,512]{2,1,0:T(8,128)(2,1)}, bf16[2,1376,512]{2,1,0:T(8,128)(2,1)S(1)}, u32[]{:S(2)}, u32[]{:S(2)}) collective-permute-start(bf16[2,1376,512]{2,1,0:T(8,128)(2,1)} %shard_map.76.after_ref), channel_id=1, source_target_pairs={{5,0},{4,1},{7,2},{6,3},{1,4},{0,5},{3,6},{2,7},{13,8},{12,9},{15,... | collective-permute-start | bytes 8454152 | tf_op jit(solution)/shard_map/ppermute | solution.py:160
  54.3 355.9 %collective-permute-start.14 = (bf16[2,1376,512]{2,1,0:T(8,128)(2,1)}, bf16[2,1376,512]{2,1,0:T(8,128)(2,1)}, u32[]{:S(2)}, u32[]{:S(2)}) collective-permute-start(bf16[2,1376,512]{2,1,0:T(8,128)(2,1)} %shard_map.77.after_ref), channel_id=1, source_target_pairs={{4,0},{5,1},{6,2},{7,3},{0,4},{1,5},{2,6},{3,7},{12,8},{13,9},{14,... | collective-permute-start | bytes 8454152 | tf_op jit(solution)/shard_map/ppermute | solution.py:160
  64.1 346.1 %collective-permute-start.8 = (bf16[256,4224]{1,0:T(8,128)(2,1)}, bf16[256,4224]{1,0:T(8,128)(2,1)}, u32[]{:S(2)}, u32[]{:S(2)}) collective-permute-start(bf16[256,4224]{1,0:T(8,128)(2,1)} %get-tuple-element.46), channel_id=1, source_target_pairs={{8,0},{0,8},{24,16},{16,24},{9,1},{1,9},{25,17},{17,25},{10,2},{2,... | collective-permute-start | bytes 6488072 | tf_op jit(solution)/shard_map/ppermute | solution.py:160
  69.5 400.7 %collective-permute-start.13 = (bf16[2,1376,512]{2,1,0:T(8,128)(2,1)}, bf16[2,1376,512]{2,1,0:T(8,128)(2,1)}, u32[]{:S(2)}, u32[]{:S(2)}) collective-permute-start(bf16[2,1376,512]{2,1,0:T(8,128)(2,1)} %shard_map.78.after_ref), channel_id=1, source_target_pairs={{7,0},{6,1},{1,2},{0,3},{3,4},{2,5},{5,6},{4,7},{15,8},{14,9},{9,1... | collective-permute-start | bytes 8454152 | tf_op jit(solution)/shard_map/ppermute | solution.py:160
  77.0 394.7 %collective-permute-start.12 = (bf16[2,1376,512]{2,1,0:T(8,128)(2,1)}, bf16[2,1376,512]{2,1,0:T(8,128)(2,1)}, u32[]{:S(2)}, u32[]{:S(2)}) collective-permute-start(bf16[2,1376,512]{2,1,0:T(8,128)(2,1)} %shard_map.79.after_ref), channel_id=1, source_target_pairs={{6,0},{7,1},{0,2},{1,3},{2,4},{3,5},{4,6},{5,7},{14,8},{15,9},{8,1... | collective-permute-start | bytes 8454152 | tf_op jit(solution)/shard_map/ppermute | solution.py:160
  349.6 65.1 %copy-start.6 = (bf16[2,1376,512]{2,1,0:T(8,128)(2,1)}, bf16[2,1376,512]{2,1,0:T(8,128)(2,1)S(1)}, u32[]{:S(2)}) copy-start(bf16[2,1376,512]{2,1,0:T(8,128)(2,1)S(1)} %collective-permute-done.15.piece_ref) | copy-start | bytes 8454148
  349.6 241.9 %collective-permute-start.11 = (bf16[2,1376,512]{2,1,0:T(8,128)(2,1)}, bf16[2,1376,512]{2,1,0:T(8,128)(2,1)}, u32[]{:S(2)}, u32[]{:S(2)}) collective-permute-start(bf16[2,1376,512]{2,1,0:T(8,128)(2,1)} %shard_map.80.after_ref), channel_id=1, source_target_pairs={{3,0},{2,1},{5,2},{4,3},{7,4},{6,5},{1,6},{0,7},{11,8},{10,9},{13,... | collective-permute-start | bytes 8454152 | tf_op jit(solution)/shard_map/ppermute | solution.py:160
  410.2 181.4 %collective-permute-start.10 = (bf16[2,1376,512]{2,1,0:T(8,128)(2,1)}, bf16[2,1376,512]{2,1,0:T(8,128)(2,1)}, u32[]{:S(2)}, u32[]{:S(2)}) collective-permute-start(bf16[2,1376,512]{2,1,0:T(8,128)(2,1)} %shard_map.81.after_ref), channel_id=1, source_target_pairs={{2,0},{3,1},{4,2},{5,3},{6,4},{7,5},{0,6},{1,7},{10,8},{11,9},{12,... | collective-permute-start | bytes 8454152 | tf_op jit(solution)/shard_map/ppermute | solution.py:160
  410.2 186.0 %collective-permute-start.9 = (bf16[2,1376,512]{2,1,0:T(8,128)(2,1)}, bf16[2,1376,512]{2,1,0:T(8,128)(2,1)}, u32[]{:S(2)}, u32[]{:S(2)}) collective-permute-start(bf16[2,1376,512]{2,1,0:T(8,128)(2,1)} %shard_map.82.after_ref), channel_id=1, source_target_pairs={{1,0},{0,1},{3,2},{2,3},{5,4},{4,5},{7,6},{6,7},{9,8},{8,9},{11,10... | collective-permute-start | bytes 8454152 | tf_op jit(solution)/shard_map/ppermute | solution.py:160
  470.2 83.3 %collective-permute-start.29 = (bf16[1,1376,384]{2,1,0:T(8,128)(2,1)}, bf16[1,1376,384]{2,1,0:T(8,128)(2,1)}, u32[]{:S(2)}, u32[]{:S(2)}) collective-permute-start(bf16[1,1376,384]{2,1,0:T(8,128)(2,1)} %shard_map.89.after_ref), channel_id=1, source_target_pairs={{1,0},{0,1},{3,2},{2,3},{5,4},{4,5},{7,6},{6,7},{9,8},{8,9},{11,10... | collective-permute-start | bytes 3170312 | tf_op jit(solution)/shard_map/ppermute | solution.py:160
  471.7 119.8 %collective-permute-start.28 = (bf16[1,1376,384]{2,1,0:T(8,128)(2,1)}, bf16[1,1376,384]{2,1,0:T(8,128)(2,1)}, u32[]{:S(2)}, u32[]{:S(2)}) collective-permute-start(bf16[1,1376,384]{2,1,0:T(8,128)(2,1)} %shard_map.88.after_ref), channel_id=1, source_target_pairs={{2,0},{3,1},{4,2},{5,3},{6,4},{7,5},{0,6},{1,7},{10,8},{11,9},{12,... | collective-permute-start | bytes 3170312 | tf_op jit(solution)/shard_map/ppermute | solution.py:160
  506.2 85.4 %copy-start.4 = (bf16[1,1376,384]{2,1,0:T(8,128)(2,1)S(1)}, bf16[1,1376,384]{2,1,0:T(8,128)(2,1)}, u32[]{:S(2)}) copy-start(bf16[1,1376,384]{2,1,0:T(8,128)(2,1)} %shard_map.86.after_ref) | copy-start | bytes 3170308
  506.2 85.4 %copy-start.3 = (bf16[1,1376,384]{2,1,0:T(8,128)(2,1)S(1)}, bf16[1,1376,384]{2,1,0:T(8,128)(2,1)}, u32[]{:S(2)}) copy-start(bf16[1,1376,384]{2,1,0:T(8,128)(2,1)} %shard_map.85.after_ref) | copy-start | bytes 3170308
  506.2 85.5 %copy-start.2 = (bf16[1,1376,384]{2,1,0:T(8,128)(2,1)S(1)}, bf16[1,1376,384]{2,1,0:T(8,128)(2,1)}, u32[]{:S(2)}) copy-start(bf16[1,1376,384]{2,1,0:T(8,128)(2,1)} %shard_map.84.after_ref) | copy-start | bytes 3170308
  553.5 69.6 %collective-permute-start.27 = (bf16[1,1376,384]{2,1,0:T(8,128)(2,1)}, bf16[1,1376,384]{2,1,0:T(8,128)(2,1)}, u32[]{:S(2)}, u32[]{:S(2)}) collective-permute-start(bf16[1,1376,384]{2,1,0:T(8,128)(2,1)} %shard_map.87.after_ref), channel_id=1, source_target_pairs={{3,0},{2,1},{5,2},{4,3},{7,4},{6,5},{1,6},{0,7},{11,8},{10,9},{13,... | collective-permute-start | bytes 3170312 | tf_op jit(solution)/shard_map/ppermute | solution.py:160
  591.6 47.3 %collective-permute-start.26 = (bf16[1,1376,384]{2,1,0:T(8,128)(2,1)S(1)}, bf16[1,1376,384]{2,1,0:T(8,128)(2,1)}, u32[]{:S(2)}, u32[]{:S(2)}) collective-permute-start(bf16[1,1376,384]{2,1,0:T(8,128)(2,1)S(1)} %copy-done.4), channel_id=1, source_target_pairs={{6,0},{7,1},{0,2},{1,3},{2,4},{3,5},{4,6},{5,7},{14,8},{15,9},{8,1... | collective-permute-start | bytes 3170312 | tf_op jit(solution)/shard_map/ppermute | solution.py:160
  591.6 70.2 %collective-permute-start.25 = (bf16[1,1376,384]{2,1,0:T(8,128)(2,1)S(1)}, bf16[1,1376,384]{2,1,0:T(8,128)(2,1)}, u32[]{:S(2)}, u32[]{:S(2)}) collective-permute-start(bf16[1,1376,384]{2,1,0:T(8,128)(2,1)S(1)} %copy-done.3), channel_id=1, source_target_pairs={{7,0},{6,1},{1,2},{0,3},{3,4},{2,5},{5,6},{4,7},{15,8},{14,9},{9,1... | collective-permute-start | bytes 3170312 | tf_op jit(solution)/shard_map/ppermute | solution.py:160
  591.7 135.8 %collective-permute-start.24 = (bf16[1,1376,384]{2,1,0:T(8,128)(2,1)S(1)}, bf16[1,1376,384]{2,1,0:T(8,128)(2,1)}, u32[]{:S(2)}, u32[]{:S(2)}) collective-permute-start(bf16[1,1376,384]{2,1,0:T(8,128)(2,1)S(1)} %copy-done.2), channel_id=1, source_target_pairs={{4,0},{5,1},{6,2},{7,3},{0,4},{1,5},{2,6},{3,7},{12,8},{13,9},{14,... | collective-permute-start | bytes 3170312 | tf_op jit(solution)/shard_map/ppermute | solution.py:160
  596.3 161.8 %collective-permute-start.23 = (bf16[1,1376,384]{2,1,0:T(8,128)(2,1)}, bf16[1,1376,384]{2,1,0:T(8,128)(2,1)}, u32[]{:S(2)}, u32[]{:S(2)}) collective-permute-start(bf16[1,1376,384]{2,1,0:T(8,128)(2,1)} %shard_map.83.after_ref), channel_id=1, source_target_pairs={{5,0},{4,1},{7,2},{6,3},{1,4},{0,5},{3,6},{2,7},{13,8},{12,9},{15,... | collective-permute-start | bytes 3170312 | tf_op jit(solution)/shard_map/ppermute | solution.py:160
  618.4 4.7 copy-start.1
  623.1 157.8 %collective-permute-start.22 = (bf16[1,1376,128]{2,1,0:T(8,128)(2,1)S(1)}, bf16[1,1376,128]{2,1,0:T(8,128)(2,1)}, u32[]{:S(2)}, u32[]{:S(2)}) collective-permute-start(bf16[1,1376,128]{2,1,0:T(8,128)(2,1)S(1)} %copy-done.1), channel_id=1, source_target_pairs={{1,0},{0,1},{3,2},{2,3},{5,4},{4,5},{7,6},{6,7},{9,8},{8,9},{11,10... | collective-permute-start | bytes 1056776 | tf_op jit(solution)/shard_map/ppermute | solution.py:160
  638.8 142.5 %collective-permute-start.21 = (bf16[1,1376,128]{2,1,0:T(8,128)(2,1)}, bf16[1,1376,128]{2,1,0:T(8,128)(2,1)S(1)}, u32[]{:S(2)}, u32[]{:S(2)}) collective-permute-start(bf16[1,1376,128]{2,1,0:T(8,128)(2,1)} %shard_map.95.after_ref), channel_id=1, source_target_pairs={{2,0},{3,1},{4,2},{5,3},{6,4},{7,5},{0,6},{1,7},{10,8},{11,9},{12,... | collective-permute-start | bytes 1056776 | tf_op jit(solution)/shard_map/ppermute | solution.py:160
  661.8 120.1 %collective-permute-start.20 = (bf16[1,1376,128]{2,1,0:T(8,128)(2,1)}, bf16[1,1376,128]{2,1,0:T(8,128)(2,1)S(1)}, u32[]{:S(2)}, u32[]{:S(2)}) collective-permute-start(bf16[1,1376,128]{2,1,0:T(8,128)(2,1)} %shard_map.94.after_ref), channel_id=1, source_target_pairs={{3,0},{2,1},{5,2},{4,3},{7,4},{6,5},{1,6},{0,7},{11,8},{10,9},{13,... | collective-permute-start | bytes 1056776 | tf_op jit(solution)/shard_map/ppermute | solution.py:160
  727.5 55.4 %collective-permute-start.19 = (bf16[1,1376,128]{2,1,0:T(8,128)(2,1)}, bf16[1,1376,128]{2,1,0:T(8,128)(2,1)S(1)}, u32[]{:S(2)}, u32[]{:S(2)}) collective-permute-start(bf16[1,1376,128]{2,1,0:T(8,128)(2,1)} %shard_map.93.after_ref), channel_id=1, source_target_pairs={{6,0},{7,1},{0,2},{1,3},{2,4},{3,5},{4,6},{5,7},{14,8},{15,9},{8,1... | collective-permute-start | bytes 1056776 | tf_op jit(solution)/shard_map/ppermute | solution.py:160
  775.1 7.9 copy-start.9
  775.1 25.9 %copy-start.8 = (bf16[1,1376,128]{2,1,0:T(8,128)(2,1)S(1)}, bf16[1,1376,128]{2,1,0:T(8,128)(2,1)}, u32[]{:S(2)}) copy-start(bf16[1,1376,128]{2,1,0:T(8,128)(2,1)} %shard_map.91.after_ref) | copy-start | bytes 1056772
  775.1 42.2 %copy-start.7 = (bf16[1,1376,128]{2,1,0:T(8,128)(2,1)S(1)}, bf16[1,1376,128]{2,1,0:T(8,128)(2,1)}, u32[]{:S(2)}) copy-start(bf16[1,1376,128]{2,1,0:T(8,128)(2,1)} %shard_map.90.after_ref) | copy-start | bytes 1056772
  775.1 71.5 %collective-permute-start.30 = (bf16[8,256,384]{2,1,0:T(8,128)(2,1)}, bf16[8,256,384]{2,1,0:T(8,128)(2,1)}, u32[]{:S(2)}, u32[]{:S(2)}) collective-permute-start(bf16[8,256,384]{2,1,0:T(8,128)(2,1)} %split.61), channel_id=1, source_target_pairs={{8,0},{0,8},{24,16},{16,24},{9,1},{1,9},{25,17},{17,25},{10,2},{2,... | collective-permute-start | bytes 4718600 | tf_op jit(solution)/shard_map/ppermute | solution.py:160
  780.9 71.0 %collective-permute-start = (bf16[2,1024,512]{2,1,0:T(8,128)(2,1)}, bf16[2,1024,512]{2,1,0:T(8,128)(2,1)}, u32[]{:S(2)}, u32[]{:S(2)}) collective-permute-start(bf16[2,1024,512]{2,1,0:T(8,128)(2,1)} %get-tuple-element.43), channel_id=1, source_target_pairs={{24,0},{0,8},{8,16},{16,24},{25,1},{1,9},{9,17},{17,25},{26,2},{2,... | collective-permute-start | bytes 6291464 | tf_op jit(solution)/shard_map/ppermute | solution.py:165
  781.3 39.3 %copy-start.11 = (bf16[1,1376,128]{2,1,0:T(8,128)(2,1)}, bf16[1,1376,128]{2,1,0:T(8,128)(2,1)S(1)}, u32[]{:S(2)}) copy-start(bf16[1,1376,128]{2,1,0:T(8,128)(2,1)S(1)} %collective-permute-done.21.refs_6_) | copy-start | bytes 1056772
  781.3 70.6 %collective-permute-start.1 = (bf16[2,1024,512]{2,1,0:T(8,128)(2,1)}, bf16[2,1024,512]{2,1,0:T(8,128)(2,1)}, u32[]{:S(2)}, u32[]{:S(2)}) collective-permute-start(bf16[2,1024,512]{2,1,0:T(8,128)(2,1)} %get-tuple-element.45), channel_id=1, source_target_pairs={{16,0},{24,8},{0,16},{8,24},{17,1},{25,9},{1,17},{9,25},{18,2},{26... | collective-permute-start | bytes 6291464 | tf_op jit(solution)/shard_map/ppermute | solution.py:165
  781.9 38.8 %copy-start.12 = (bf16[1,1376,128]{2,1,0:T(8,128)(2,1)}, bf16[1,1376,128]{2,1,0:T(8,128)(2,1)S(1)}, u32[]{:S(2)}) copy-start(bf16[1,1376,128]{2,1,0:T(8,128)(2,1)S(1)} %collective-permute-done.20.refs_5_) | copy-start | bytes 1056772
  781.9 91.3 %collective-permute-start.2 = (bf16[2,1024,512]{2,1,0:T(8,128)(2,1)}, bf16[2,1024,512]{2,1,0:T(8,128)(2,1)}, u32[]{:S(2)}, u32[]{:S(2)}) collective-permute-start(bf16[2,1024,512]{2,1,0:T(8,128)(2,1)} %get-tuple-element.44), channel_id=1, source_target_pairs={{8,0},{16,8},{24,16},{0,24},{9,1},{17,9},{25,17},{1,25},{10,2},{18... | collective-permute-start | bytes 6291464 | tf_op jit(solution)/shard_map/ppermute | solution.py:165
  782.9 37.7 %copy-start.13 = (bf16[1,1376,128]{2,1,0:T(8,128)(2,1)}, bf16[1,1376,128]{2,1,0:T(8,128)(2,1)S(1)}, u32[]{:S(2)}) copy-start(bf16[1,1376,128]{2,1,0:T(8,128)(2,1)S(1)} %collective-permute-done.19.refs_4_) | copy-start | bytes 1056772
  782.9 18.0 %collective-permute-start.18 = (bf16[1,1376,128]{2,1,0:T(8,128)(2,1)S(1)}, bf16[1,1376,128]{2,1,0:T(8,128)(2,1)S(1)}, u32[]{:S(2)}, u32[]{:S(2)}) collective-permute-start(bf16[1,1376,128]{2,1,0:T(8,128)(2,1)S(1)} %copy-done.9), channel_id=1, source_target_pairs={{7,0},{6,1},{1,2},{0,3},{3,4},{2,5},{5,6},{4,7},{15,8},{14,9},{9,1... | collective-permute-start | bytes 1056776 | tf_op jit(solution)/shard_map/ppermute | solution.py:160
  801.0 19.7 %copy-start.14 = (bf16[1,1376,128]{2,1,0:T(8,128)(2,1)}, bf16[1,1376,128]{2,1,0:T(8,128)(2,1)S(1)}, u32[]{:S(2)}) copy-start(bf16[1,1376,128]{2,1,0:T(8,128)(2,1)S(1)} %collective-permute-done.18.refs_3_) | copy-start | bytes 1056772
  801.0 16.3 %collective-permute-start.17 = (bf16[1,1376,128]{2,1,0:T(8,128)(2,1)S(1)}, bf16[1,1376,128]{2,1,0:T(8,128)(2,1)S(1)}, u32[]{:S(2)}, u32[]{:S(2)}) collective-permute-start(bf16[1,1376,128]{2,1,0:T(8,128)(2,1)S(1)} %copy-done.8), channel_id=1, source_target_pairs={{4,0},{5,1},{6,2},{7,3},{0,4},{1,5},{2,6},{3,7},{12,8},{13,9},{14,... | collective-permute-start | bytes 1056776 | tf_op jit(solution)/shard_map/ppermute | solution.py:160
  817.3 3.3 copy-start.15
  817.3 18.7 %collective-permute-start.16 = (bf16[1,1376,128]{2,1,0:T(8,128)(2,1)S(1)}, bf16[1,1376,128]{2,1,0:T(8,128)(2,1)S(1)}, u32[]{:S(2)}, u32[]{:S(2)}) collective-permute-start(bf16[1,1376,128]{2,1,0:T(8,128)(2,1)S(1)} %copy-done.7), channel_id=1, source_target_pairs={{5,0},{4,1},{7,2},{6,3},{1,4},{0,5},{3,6},{2,7},{13,8},{12,9},{15,... | collective-permute-start | bytes 1056776 | tf_op jit(solution)/shard_map/ppermute | solution.py:160
  836.0 0.7 copy-start.16
  836.7 9.9 %copy-start.5 = (bf16[8,512,384]{2,1,0:T(8,128)(2,1)S(1)}, bf16[8,512,384]{2,1,0:T(8,128)(2,1)}, u32[]{:S(2)}) copy-start(bf16[8,512,384]{2,1,0:T(8,128)(2,1)} %get-tuple-element.41) | copy-start | bytes 9437188
  846.5 2.7 collective-permute-start.36
  846.6 2.7 copy-start.10
  848.6 49.0 %collective-permute-start.31 = (bf16[8,128,384]{2,1,0:T(8,128)(2,1)S(1)}, bf16[8,128,384]{2,1,0:T(8,128)(2,1)S(1)}, u32[]{:S(2)}, u32[]{:S(2)}) collective-permute-start(bf16[8,128,384]{2,1,0:T(8,128)(2,1)S(1)} %split.81), channel_id=1, source_target_pairs={{16,0},{24,8},{0,16},{8,24},{17,1},{25,9},{1,17},{9,25},{18,2},{26... | collective-permute-start | bytes 2359304 | tf_op jit(solution)/shard_map/ppermute | solution.py:160
  850.4 46.0 %collective-permute-start.37 = (bf16[8,128,128]{2,1,0:T(8,128)(2,1)S(1)}, bf16[8,128,128]{2,1,0:T(8,128)(2,1)S(1)}, u32[]{:S(2)}, u32[]{:S(2)}) collective-permute-start(bf16[8,128,128]{2,1,0:T(8,128)(2,1)S(1)} %split.89), channel_id=1, source_target_pairs={{16,0},{24,8},{0,16},{8,24},{17,1},{25,9},{1,17},{9,25},{18,2},{26... | collective-permute-start | bytes 786440 | tf_op jit(solution)/shard_map/ppermute | solution.py:160
  896.5 6.4 collective-permute-start.38
  897.9 14.2 %collective-permute-start.32 = (bf16[8,64,384]{2,1,0:T(8,128)(2,1)S(1)}, bf16[8,64,384]{2,1,0:T(8,128)(2,1)S(1)}, u32[]{:S(2)}, u32[]{:S(2)}) collective-permute-start(bf16[8,64,384]{2,1,0:T(8,128)(2,1)S(1)} %split.83), channel_id=1, source_target_pairs={{1,0},{0,1},{3,2},{2,3},{5,4},{4,5},{7,6},{6,7},{9,8},{8,9},{11,10... | collective-permute-start | bytes 1179656 | tf_op jit(solution)/shard_map/ppermute | solution.py:160
  903.0 16.1 %collective-permute-start.39 = (bf16[8,16,128]{2,1,0:T(8,128)(2,1)S(1)}, bf16[8,16,128]{2,1,0:T(8,128)(2,1)S(1)}, u32[]{:S(2)}, u32[]{:S(2)}) collective-permute-start(bf16[8,16,128]{2,1,0:T(8,128)(2,1)S(1)} %get-tuple-element.67), channel_id=1, source_target_pairs={{6,0},{7,1},{0,2},{1,3},{2,4},{3,5},{4,6},{5,7},{14,8},{15,9},{8,1... | collective-permute-start | bytes 98312 | tf_op jit(solution)/shard_map/ppermute | solution.py:160
  909.1 10.1 %collective-permute-start.40 = (bf16[8,16,128]{2,1,0:T(8,128)(2,1)S(1)}, bf16[8,16,128]{2,1,0:T(8,128)(2,1)S(1)}, u32[]{:S(2)}, u32[]{:S(2)}) collective-permute-start(bf16[8,16,128]{2,1,0:T(8,128)(2,1)S(1)} %get-tuple-element.69), channel_id=1, source_target_pairs={{4,0},{5,1},{6,2},{7,3},{0,4},{1,5},{2,6},{3,7},{12,8},{13,9},{14,... | collective-permute-start | bytes 98312 | tf_op jit(solution)/shard_map/ppermute | solution.py:160
  912.0 7.2 collective-permute-start.41
  912.2 10.2 %collective-permute-start.33 = (bf16[8,16,384]{2,1,0:T(8,128)(2,1)S(1)}, bf16[8,16,384]{2,1,0:T(8,128)(2,1)S(1)}, u32[]{:S(2)}, u32[]{:S(2)}) collective-permute-start(bf16[8,16,384]{2,1,0:T(8,128)(2,1)S(1)} %get-tuple-element.51), channel_id=1, source_target_pairs={{6,0},{7,1},{0,2},{1,3},{2,4},{3,5},{4,6},{5,7},{14,8},{15,9},{8,1... | collective-permute-start | bytes 294920 | tf_op jit(solution)/shard_map/ppermute | solution.py:160
  915.7 9.0 collective-permute-start.34
  919.2 6.0 collective-permute-start.35
